TPU v7x, 32 devices: a whole 2x2x4 slice. The times are simulated.
32 devices in a mesh: grp: 2 (over x), dom: 16 (over z, y, core).
Axes of the slice: x: 2, y: 2, z: 4, core: 2. Of those that a mesh axis runs over, the one named last changes fastest.
Arguments:
- positions: float32 [512, 3, 128], P(('grp', 'dom')), may hold values from 0 to 1
- smoothing: float32 [512, 128], P(('grp', 'dom')), may hold values from 0.35 to 0.55
- energy: float32 [512, 128], P(('grp', 'dom')), may hold values from 0.5 to 2
- mass: float32 [512, 128], P(('grp', 'dom')), may hold values from 0.00390625 to 0.015625
- old_density: float32 [512, 128], P(('grp', 'dom')), may hold values from 1 to 6
- active: int32 [512, 128], P(('grp', 'dom')), may hold values 0 or 1
- pair_list: int32 [512, 2], P(('grp', 'dom')), may hold values from 0 to 15
- export_leaves: int32 [768, 2], P(('grp', 'dom')), may hold values from 0 to 15
- export_route: int32 [768, 1], P(('grp', 'dom')), may hold values from 0 to 14; in each aligned block of 24 rows (0 to 23, 24 to 47, ...) at most 2 rows name the same one
Outputs:
- density: float32 [512, 128], P(('grp', 'dom'))
- acceleration: float32 [512, 3, 128], P(('grp', 'dom'))
- timestep: float32 [], replicated
Inputs may be any that keep to these rules, and one draw needn't show every extreme that they name: `pair_list`: indices of leaf blocks of the domain that holds the row. `export_leaves`: column 0 is a leaf block of the domain that holds the row, column 1 a leaf block of the destination domain. `export_route`: among the rows of one domain no value occurs more than 2 times; in some domains one value occurs exactly 2 times. `active`: every domain holds some particles with value 1.
All inputs are finite; a program needn't handle non-finite values. No bound on the sum of `active` on one device may be relied on, other than what follows from the above.
Results may differ from a plain program's by a relative error of at most 0.0003.
Values sent between devices are 32-bit elements; how exact they have to be, the bound alone decides.
No kernel may reach another device: no remote copies, remote signals or barrier semaphores. Data moves between devices by JAX's collectives and lax.ppermute only.
A program may use at most 64 MiB of HBM per device.

v0:
```python
import math
import jax
import jax.numpy as jnp
from jax import lax
from jax.sharding import PartitionSpec as P

MOST = 2
ADIABATIC = 5.0 / 3.0
COURANT = 0.3
batch_tiles = 8


def kernel_value(dist, smooth):
    ratio = dist / smooth
    inner = 1.0 - 6.0 * ratio * ratio + 6.0 * ratio * ratio * ratio
    remain = jnp.maximum(1.0 - ratio, 0.0)
    outer = 2.0 * remain * remain * remain
    return jnp.where(ratio < 0.5, inner, outer) * (8.0 / math.pi) / (smooth * smooth * smooth)


def kernel_slope(dist, smooth):
    ratio = dist / smooth
    inner = -12.0 + 18.0 * ratio
    remain = jnp.maximum(1.0 - ratio, 0.0)
    outer = -6.0 * remain * remain / jnp.maximum(ratio, 0.5)
    square = smooth * smooth
    return jnp.where(ratio < 0.5, inner, outer) * (8.0 / math.pi) / (square * square * smooth)


def density_tile(own_pos, own_h, far_pos, far_mass):
    offset = own_pos[:, :, None] - far_pos[:, None, :]
    dist = jnp.sqrt(jnp.sum(offset * offset, axis=0))
    return jnp.sum(kernel_value(dist, own_h[:, None]) * far_mass[None, :], axis=1)


def force_tile(own_pos, own_h, own_term, far_pos, far_h, far_mass, far_term):
    offset = own_pos[:, :, None] - far_pos[:, None, :]
    dist = jnp.sqrt(jnp.sum(offset * offset, axis=0))
    slope = 0.5 * (kernel_slope(dist, own_h[:, None]) + kernel_slope(dist, far_h[None, :]))
    weight = far_mass[None, :] * (own_term[:, None] + far_term[None, :]) * slope
    return -jnp.sum(weight[None, :, :] * offset, axis=2)


def blockwise(kernel, operands):
    count = operands[0].shape[0]
    width = min(batch_tiles, count)
    shaped = tuple((item.reshape((count // width, width) + item.shape[1:]) for item in operands))
    result = lax.map(lambda group: jax.vmap(kernel)(*group), shaped)
    return result.reshape((count,) + result.shape[2:])


def collect(owner, values):
    flat = values.reshape(values.shape[0], -1)
    total = jnp.dot(
        owner, flat, precision=lax.Precision.HIGHEST, preferred_element_type=jnp.float32
    )
    return total.reshape((owner.shape[0],) + values.shape[1:])


def body(
    positions, smoothing, energy, mass, old_density, active, pair_list, export_leaves, export_route
):
    leaves = positions.shape[0]
    width = positions.shape[2]
    exported = export_leaves.shape[0]
    domains = lax.axis_size("dom")
    myself = lax.axis_index("dom")
    slots = domains * MOST
    target_dom = (myself + 1 + export_route[:, 0]) % domains
    columns = jnp.arange(domains, dtype=jnp.int32)
    onehot = (target_dom[:, None] == columns[None, :]).astype(jnp.int32)
    earlier = jnp.cumsum(onehot, axis=0) - onehot
    rank_in = jnp.sum(earlier * onehot, axis=1)
    slot_of = target_dom * MOST + rank_in
    match = (slot_of[None, :] == jnp.arange(slots, dtype=jnp.int32)[:, None]).astype(jnp.int32)
    filled = jnp.sum(match, axis=1) > 0
    chosen = jnp.sum(match * jnp.arange(exported, dtype=jnp.int32)[None, :], axis=1)
    send_leaf = export_leaves[chosen, 0]
    send_target = jnp.where(filled, export_leaves[chosen, 1], 0)
    leaf_ids = jnp.arange(leaves, dtype=jnp.int32)
    slot_owner = ((send_leaf[None, :] == leaf_ids[:, None]) & filled[None, :]).astype(jnp.float32)
    pair_owner = (pair_list[None, :, 0] == leaf_ids[:, None]).astype(jnp.float32)
    own_idx = pair_list[:, 0]
    far_idx = pair_list[:, 1]
    send_pos = positions[send_leaf]
    send_h = smoothing[send_leaf]
    wanted = lax.all_to_all(
        send_target.reshape(domains, MOST), "dom", split_axis=0, concat_axis=0, tiled=True
    )
    wanted = wanted.reshape(slots)
    served = jnp.concatenate(
        [positions[wanted], smoothing[wanted][:, None, :], mass[wanted][:, None, :]], axis=1
    )
    fetched = lax.all_to_all(
        served.reshape(domains, MOST, 5, width), "dom", split_axis=0, concat_axis=0, tiled=True
    )
    fetched = fetched.reshape(slots, 5, width)
    remote_density = collect(
        slot_owner, blockwise(density_tile, (send_pos, send_h, fetched[:, 0:3], fetched[:, 4]))
    )
    local_part = blockwise(
        density_tile, (positions[own_idx], smoothing[own_idx], positions[far_idx], mass[far_idx])
    )
    self_term = mass * kernel_value(jnp.zeros_like(smoothing), smoothing)
    summed = collect(pair_owner, local_part) + remote_density
    density = jnp.where(active == 1, self_term + summed, old_density)
    term = (ADIABATIC - 1.0) * energy / density
    far_term = lax.all_to_all(
        term[wanted].reshape(domains, MOST, width), "dom", split_axis=0, concat_axis=0, tiled=True
    )
    far_term = far_term.reshape(slots, width)
    remote_force = blockwise(
        force_tile,
        (
            send_pos,
            send_h,
            term[send_leaf],
            fetched[:, 0:3],
            fetched[:, 3],
            fetched[:, 4],
            far_term,
        ),
    )
    remote_accel = collect(slot_owner, remote_force)
    local_force = blockwise(
        force_tile,
        (
            positions[own_idx],
            smoothing[own_idx],
            term[own_idx],
            positions[far_idx],
            smoothing[far_idx],
            mass[far_idx],
            term[far_idx],
        ),
    )
    accel = collect(pair_owner, local_force) + remote_accel
    acceleration = jnp.where((active == 1)[:, None, :], accel, 0.0)
    speed = jnp.sqrt(ADIABATIC * (ADIABATIC - 1.0) * energy)
    magnitude = jnp.sqrt(jnp.sum(acceleration * acceleration, axis=1))
    step_size = COURANT * smoothing / (speed + jnp.sqrt(smoothing * magnitude))
    local_least = jnp.min(jnp.where(active == 1, step_size, jnp.inf))
    timestep = lax.pmin(local_least, ("grp", "dom"))
    return (density, acceleration, timestep)


def solution(mesh):
    return jax.shard_map(
        body,
        mesh=mesh,
        in_specs=(
            P(("grp", "dom"), None, None),
            P(("grp", "dom"), None),
            P(("grp", "dom"), None),
            P(("grp", "dom"), None),
            P(("grp", "dom"), None),
            P(("grp", "dom"), None),
            P(("grp", "dom"), None),
            P(("grp", "dom"), None),
            P(("grp", "dom"), None),
        ),
        out_specs=(P(("grp", "dom"), None), P(("grp", "dom"), None, None), P()),
        check_vma=False,
    )
```

profile of v0, /device:TPU:0, one launch (start us, length us, event | category | flops | bytes accessed | tf_op | source)
XLA Modules:
  0.0 107.7 jit_solution(8637589466511635926)
XLA Ops:
  0.7 0.7 fusion.71
  1.7 0.7 fusion.70
  2.4 1.4 %gather_fusion.6 = s32[32]{0:T(128)S(1)} fusion(s32[24,2]{0,1:T(2,128)} %param.24, s32[32]{0:T(128)S(1)} %get-tuple-element.380), kind=kCustom, calls=%fused_computation.6 | custom fusion | bytes 512 | tf_op jit(solution)/shard_map/gather | solution.py:79
  3.9 0.7 select_n.140
  4.6 7.4 %all-to-all-start = ((s32[16,1,2]{2,1,0:T(1,128)}), s32[16,1,2]{2,1,0:T(1,128)S(1)}, u32[]{:S(2)}, u32[]{:S(2)}) async-start(s32[16,1,2]{2,1,0:T(1,128)} %bitcast.42), calls=%async_computation | async-start | bytes 16384 | tf_op jit(solution)/shard_map/all_to_all | solution.py:87
  12.1 0.6 gather_fusion
  13.2 0.8 gather_fusion.4
  14.0 0.6 gather_fusion.5
  14.7 0.6 gather_fusion.10
  15.2 0.6 gather_fusion.1
  16.5 0.6 gather_fusion.3
  17.0 2.3 %while.40 = (s32[]{:T(128)}, f32[2,8,128]{2,1,0:T(8,128)S(1)}, f32[2,8,3,128]{3,2,1,0:T(4,128)S(1)}, f32[2,8,3,128]{3,2,1,0:T(4,128)S(1)}, f32[2,8,128]{2,1,0:T(8,128)S(1)}, /*index=5*/f32[2,8,128]{2,1,0:T(8,128)S(1)}, s32[]{:T(128)}) while((s32[]{:T(128)}, f32[2,8,128]{2,1,0:T(8,128)S(1)}, f32[2,8,3,128]{3,2,1,0:T(4,128)S(1)}, ...), condition=%wide.region_3.4_spmd, body=%wide.region_0.0_spmd.sunk | while | flops 3277826 | bytes 1167461 | solution.py:48
  17.6 0.6 fusion.88
  18.7 0.6 fusion.88
  20.0 0.7 reduce.3
  20.8 0.6 gather_fusion.9
  21.4 0.6 gather_fusion.8
  22.0 0.6 gather_fusion.7
  22.6 0.7 pad_maximum_fusion
  23.2 6.0 %all-to-all-start.1 = ((f32[16,2,5,128]{3,1,2,0:T(2,128)}), f32[16,2,5,128]{3,1,2,0:T(2,128)S(1)}, u32[]{:S(2)}, u32[]{:S(2)}) async-start(f32[16,2,5,128]{3,1,2,0:T(2,128)} %pad_maximum_fusion), calls=%async_computation.1 | async-start | bytes 163840 | tf_op jit(solution)/shard_map/all_to_all | solution.py:94
  29.3 7.1 %all-to-all-done.1 = f32[16,2,5,128]{3,1,2,0:T(2,128)S(1)} async-done(((f32[16,2,5,128]{3,1,2,0:T(2,128)}), f32[16,2,5,128]{3,1,2,0:T(2,128)S(1)}, u32[]{:S(2)}, u32[]{:S(2)}) %all-to-all-start.1) | async-done | bytes 81952 | tf_op jit(solution)/shard_map/all_to_all | solution.py:94
  36.5 4.6 %while.41 = (s32[]{:T(128)}, f32[4,8,128]{2,1,0:T(8,128)S(1)}, f32[4,8,3,128]{3,2,1,0:T(4,128)S(1)}, f32[4,8,3,128]{3,2,1,0:T(4,128)S(1)}, f32[4,8,128]{2,1,0:T(8,128)S(1)}, /*index=5*/f32[4,8,128]{2,1,0:T(8,128)S(1)}, s32[]{:T(128)}) while((s32[]{:T(128)}, f32[4,8,128]{2,1,0:T(8,128)S(1)}, f32[4,8,3,128]{3,2,1,0:T(4,128)S(1)}, ...), condition=%wide.region_11.12_spmd, body=%wide.region_8.11_spmd.sunk | while | flops 3277826 | bytes 1167461 | solution.py:48
  37.0 0.6 fusion.89
  38.2 0.6 fusion.89
  39.3 0.6 fusion.89
  40.5 0.6 fusion.89
  41.1 0.7 multiply_divide_fusion
  42.9 1.2 %gather_fusion.15 = f32[32,128]{1,0:T(8,128)} fusion(f32[16,128]{1,0:T(8,128)S(1)} %get-tuple-element.382, s32[1024]{0:T(1024)S(1)} %pad_clamp_fusion), kind=kCustom, calls=%fused_computation.15 | custom fusion | bytes 32896 | tf_op jit(solution)/shard_map/gather | solution.py:109
  44.1 4.6 %while.42 = (s32[]{:T(128)}, f32[2,8,3,128]{3,2,1,0:T(4,128)S(1)}, f32[2,8,128]{2,1,0:T(8,128)S(1)}, f32[2,8,128]{2,1,0:T(8,128)S(1)}, f32[2,8,128]{2,1,0:T(8,12...) while((s32[]{:T(128)}, f32[2,8,3,128]{3,2,1,0:T(4,128)S(1)}, ...), condition=%wide.region_15.16_spmd, body=%wide.region_12.15_spmd.sunk | while | flops 6297602 | bytes 2318465 | solution.py:48
  44.7 0.8 multiply_multiply_fusion.28
  45.4 1.0 fusion.91
  47.0 0.8 multiply_multiply_fusion.28
  47.8 1.0 fusion.91
  48.7 3.5 %all-to-all-start.2 = ((f32[16,2,128]{2,1,0:T(2,128)}), f32[16,2,128]{2,1,0:T(2,128)S(1)}, u32[]{:S(2)}, u32[]{:S(2)}) async-start(f32[16,2,128]{2,1,0:T(2,128)} %bitcast.61), calls=%async_computation.2 | async-start | bytes 32768 | tf_op jit(solution)/shard_map/all_to_all | solution.py:108
  52.4 0.6 gather_fusion.14
  53.0 5.8 %all-to-all-done.2 = f32[16,2,128]{2,1,0:T(2,128)S(1)} async-done(((f32[16,2,128]{2,1,0:T(2,128)}), f32[16,2,128]{2,1,0:T(2,128)S(1)}, u32[]{:S(2)}, u32[]{:S(2)}) %all-to-all-start.2) | async-done | bytes 16416 | tf_op jit(solution)/shard_map/all_to_all | solution.py:108
  58.7 9.3 %while.43 = (s32[]{:T(128)}, f32[4,8,3,128]{3,2,1,0:T(4,128)S(1)}, f32[4,8,128]{2,1,0:T(8,128)S(1)}, f32[4,8,128]{2,1,0:T(8,128)S(1)}, f32[4,8,128]{2,1,0:T(8,12...) while((s32[]{:T(128)}, f32[4,8,3,128]{3,2,1,0:T(4,128)S(1)}, ...), condition=%wide.region_19.20_spmd, body=%wide.region_16.19_spmd.sunk | while | flops 6297602 | bytes 2318465 | solution.py:48
  59.3 0.8 multiply_multiply_fusion.30
  60.1 1.0 fusion.93
  61.6 0.8 multiply_multiply_fusion.30
  62.4 1.0 fusion.93
  63.9 0.8 multiply_multiply_fusion.30
  64.7 1.0 fusion.93
  66.3 0.8 multiply_multiply_fusion.30
  67.0 1.0 fusion.93
  68.0 0.8 multiply_reduce_fusion.2
  68.8 0.6 select_reduce_fusion.2
  69.4 38.3 %pmin.7 = f32[]{:T(128)} all-reduce(f32[]{:T(128)} %select_reduce_fusion.2), channel_id=1, replica_groups=mesh['grp'=2,'dom'=16] {'grp','dom'}, use_global_device_ids=true, to_apply=%region_22.23 | all-reduce | flops 1 | bytes 8 | tf_op jit(solution)/shard_map/pmin | solution.py:143
  (116 shorter events, 10.0 us)
Async XLA Ops:
  0.6 11.4 %copy-start = (f32[16,3,128]{2,0,1:T(8,128)S(1)}, f32[16,3,128]{2,0,1:T(8,128)}, u32[]{:S(2)}) copy-start(f32[16,3,128]{2,0,1:T(8,128)} %param.17) | copy-start | bytes 73732
  0.6 12.6 %copy-start.1 = (s32[24,2]{0,1:T(2,128)S(1)}, s32[24,2]{0,1:T(2,128)}, u32[]{:S(2)}) copy-start(s32[24,2]{0,1:T(2,128)} %param.24) | copy-start | bytes 580
  0.7 11.4 %copy-start.6 = (s32[16,2]{0,1:T(2,128)S(1)}, s32[16,2]{0,1:T(2,128)}, u32[]{:S(2)}) copy-start(s32[16,2]{0,1:T(2,128)} %param.23) | copy-start | bytes 388
  0.7 12.0 %copy-start.2 = (f32[16,128]{1,0:T(8,128)S(1)}, f32[16,128]{1,0:T(8,128)}, u32[]{:S(2)}) copy-start(f32[16,128]{1,0:T(8,128)} %param.18) | copy-start | bytes 24580
  4.6 14.9 %all-to-all-start = ((s32[16,1,2]{2,1,0:T(1,128)}), s32[16,1,2]{2,1,0:T(1,128)S(1)}, u32[]{:S(2)}, u32[]{:S(2)}) async-start(s32[16,1,2]{2,1,0:T(1,128)} %bitcast.42), calls=%async_computation | async-start | bytes 16384 | tf_op jit(solution)/shard_map/all_to_all | solution.py:87
  14.0 2.4 %copy-start.4 = (s32[16,128]{1,0:T(8,128)S(1)}, s32[16,128]{1,0:T(8,128)}, u32[]{:S(2)}) copy-start(s32[16,128]{1,0:T(8,128)} %param.22) | copy-start | bytes 24580
  14.0 2.4 %copy-start.3 = (f32[16,128]{1,0:T(8,128)S(1)}, f32[16,128]{1,0:T(8,128)}, u32[]{:S(2)}) copy-start(f32[16,128]{1,0:T(8,128)} %param.20) | copy-start | bytes 24580
  23.2 13.1 %all-to-all-start.1 = ((f32[16,2,5,128]{3,1,2,0:T(2,128)}), f32[16,2,5,128]{3,1,2,0:T(2,128)S(1)}, u32[]{:S(2)}, u32[]{:S(2)}) async-start(f32[16,2,5,128]{3,1,2,0:T(2,128)} %pad_maximum_fusion), calls=%async_computation.1 | async-start | bytes 163840 | tf_op jit(solution)/shard_map/all_to_all | solution.py:94
  36.5 4.6 %copy-start.5 = (f32[16,128]{1,0:T(8,128)S(1)}, f32[16,128]{1,0:T(8,128)}, u32[]{:S(2)}) copy-start(f32[16,128]{1,0:T(8,128)} %param.19) | copy-start | bytes 24580
  36.5 4.6 %copy-start.7 = (f32[16,128]{1,0:T(8,128)S(1)}, f32[16,128]{1,0:T(8,128)}, u32[]{:S(2)}) copy-start(f32[16,128]{1,0:T(8,128)} %param.21) | copy-start | bytes 24580
  48.7 10.0 %all-to-all-start.2 = ((f32[16,2,128]{2,1,0:T(2,128)}), f32[16,2,128]{2,1,0:T(2,128)S(1)}, u32[]{:S(2)}, u32[]{:S(2)}) async-start(f32[16,2,128]{2,1,0:T(2,128)} %bitcast.61), calls=%async_computation.2 | async-start | bytes 32768 | tf_op jit(solution)/shard_map/all_to_all | solution.py:108
where the time goes:
time: 108 us
  blocking collectives  38.3 us (35%)
  other arithmetic  23.5 us (22%)
  starting transfers between devices  16.9 us (16%)
  waiting for transfers between devices  12.9 us (12%)
  local copies, waits for them, and re-layouts  12.7 us (12%)
  matrix products  1.74 us (2%)
    pmin x1, blocking collectives, body(): timestep = lax.pmin(local_least, ('grp', 'dom'))  38.3 us
    all_to_all x1, starting transfers between devices, body(): lax.all_to_all(send_target.reshape(domains, MOST), 'dom', split_axis=0, c...  7.41 us
    all_to_all x1, waiting for transfers between devices, body(): lax.all_to_all(served.reshape(domains, MOST, 5, width), 'dom', split_axis...  7.1 us
    all_to_all x1, starting transfers between devices, body(): lax.all_to_all(served.reshape(domains, MOST, 5, width), 'dom', split_axis...  6 us
    all_to_all x1, waiting for transfers between devices, body(): lax.all_to_all(term[wanted].reshape(domains, MOST, width), 'dom', split_a...  5.75 us
    reduce_sum x6, other arithmetic, force_tile(): return -jnp.sum(weight[None, :, :] * offset, axis=2)  5.74 us
    mul x6, other arithmetic, force_tile(): weight = far_mass[None, :] * (own_term[:, None] + far_term[None, :]) * slope  4.61 us
    all_to_all x1, starting transfers between devices, body(): lax.all_to_all(term[wanted].reshape(domains, MOST, width), 'dom', split_a...  3.51 us
  transfers between devices with their start and end apart: 3, of which 2 were waited for; matrix products, arithmetic and copies ran while one was open for 7% of the time, Pallas kernels for 0%

commit v1 on v0

--- a/solution.py
+++ b/solution.py
@@ -8,6 +8,18 @@
 ADIABATIC = 5.0 / 3.0
 COURANT = 0.3
 batch_tiles = 8
+
+
+def exchange_directly(x, axis, split, join):
+    ways, here = (lax.axis_size(axis), lax.axis_index(axis))
+    width = x.shape[split] // ways
+    turned = jnp.roll(x, -here * width, axis=split)
+    got = [lax.slice_in_dim(turned, 0, width, axis=split)]
+    for far in range(1, ways):
+        sent = lax.slice_in_dim(turned, far * width, (far + 1) * width, axis=split)
+        got.append(lax.ppermute(sent, axis, [(d, (d + far) % ways) for d in range(ways)]))
+    line = jnp.concatenate(got[::-1], axis=join)
+    return jnp.roll(line, (here + 1) * got[0].shape[join], axis=join)
 
 
 def kernel_value(dist, smooth):
@@ -91,9 +103,7 @@
     served = jnp.concatenate(
         [positions[wanted], smoothing[wanted][:, None, :], mass[wanted][:, None, :]], axis=1
     )
-    fetched = lax.all_to_all(
-        served.reshape(domains, MOST, 5, width), "dom", split_axis=0, concat_axis=0, tiled=True
-    )
+    fetched = exchange_directly(served.reshape(domains, MOST, 5, width), "dom", 0, 0)
     fetched = fetched.reshape(slots, 5, width)
     remote_density = collect(
         slot_owner, blockwise(density_tile, (send_pos, send_h, fetched[:, 0:3], fetched[:, 4]))

time: 108 us -> 121 us (1.12)
  starting transfers between devices: 16.9 us -> 31.7 us
  waiting for transfers between devices: 12.9 us -> 11.5 us
    ppermute x0 -> x15, starting transfers between devices: none -> 20.8 us  [exchange_directly(): lax.ppermute(sent, axis, [(d, (d + far) % ways) for d in range(ways)])]
    all_to_all x1 -> x0, waiting for transfers between devices: 7.1 us -> none  [body(): lax.all_to_all(served.reshape(domains, MOST, 5, width), 'dom', split_axis...]
    all_to_all x1 -> x0, starting transfers between devices: 6 us -> none  [body(): lax.all_to_all(served.reshape(domains, MOST, 5, width), 'dom', split_axis...]
    ppermute x0 -> x15, waiting for transfers between devices: none -> 5.7 us  [exchange_directly(): lax.ppermute(sent, axis, [(d, (d + far) % ways) for d in range(ways)])]
  transfers between devices with their start and end apart: 3 -> 17, of which waited for: 2 -> 6; matrix products, arithmetic and copies ran while one was open for 7% -> 7% of each run, Pallas kernels for 0% -> 0%
where the time goes in v1:
time: 121 us
  blocking collectives  38.3 us (32%)
  starting transfers between devices  31.7 us (26%)
  other arithmetic  23 us (19%)
  local copies, waits for them, and re-layouts  12.9 us (11%)
  waiting for transfers between devices  11.5 us (10%)
  matrix products  1.74 us (1%)
    pmin x1, blocking collectives, body(): timestep = lax.pmin(local_least, ('grp', 'dom'))  38.3 us
    ppermute x15, starting transfers between devices, exchange_directly(): lax.ppermute(sent, axis, [(d, (d + far) % ways) for d in range(ways)])  20.8 us
    all_to_all x1, starting transfers between devices, body(): lax.all_to_all(send_target.reshape(domains, MOST), 'dom', split_axis=0, c...  7.41 us
    all_to_all x1, waiting for transfers between devices, body(): lax.all_to_all(term[wanted].reshape(domains, MOST, width), 'dom', split_a...  5.75 us
    reduce_sum x6, other arithmetic, force_tile(): return -jnp.sum(weight[None, :, :] * offset, axis=2)  5.74 us
    ppermute x15, waiting for transfers between devices, exchange_directly(): lax.ppermute(sent, axis, [(d, (d + far) % ways) for d in range(ways)])  5.7 us
    mul x6, other arithmetic, force_tile(): weight = far_mass[None, :] * (own_term[:, None] + far_term[None, :]) * slope  4.61 us
    all_to_all x1, starting transfers between devices, body(): lax.all_to_all(term[wanted].reshape(domains, MOST, width), 'dom', split_a...  3.51 us
  transfers between devices with their start and end apart: 17, of which 6 were waited for; matrix products, arithmetic and copies ran while one was open for 7% of the time, Pallas kernels for 0%

profile of v1, /device:TPU:0, one launch (start us, length us, event | category | flops | bytes accessed | tf_op | source)
XLA Modules:
  0.0 121.0 jit_solution(3737744499724833655)
XLA Ops:
  0.7 0.7 fusion.77
  1.6 0.7 fusion.76
  2.4 1.4 %gather_fusion.6 = s32[32]{0:T(128)S(1)} fusion(s32[24,2]{0,1:T(2,128)} %param.26, s32[32]{0:T(128)S(1)} %get-tuple-element.366), kind=kCustom, calls=%fused_computation.6 | custom fusion | bytes 512 | tf_op jit(solution)/shard_map/gather | solution.py:91
  3.9 0.7 select_n.149
  4.6 7.4 %all-to-all-start = ((s32[16,1,2]{2,1,0:T(1,128)}), s32[16,1,2]{2,1,0:T(1,128)S(1)}, u32[]{:S(2)}, u32[]{:S(2)}) async-start(s32[16,1,2]{2,1,0:T(1,128)} %bitcast.42), calls=%async_computation | async-start | bytes 16384 | tf_op jit(solution)/shard_map/all_to_all | solution.py:99
  12.1 0.6 gather_fusion
  12.7 0.6 gather_fusion.1
  15.1 2.3 %while.40 = (s32[]{:T(128)}, f32[2,8,128]{2,1,0:T(8,128)S(1)}, f32[2,8,3,128]{3,2,1,0:T(4,128)S(1)}, f32[2,8,3,128]{3,2,1,0:T(4,128)S(1)}, f32[2,8,128]{2,1,0:T(8,128)S(1)}, /*index=5*/f32[2,8,128]{2,1,0:T(8,128)S(1)}, s32[]{:T(128)}) while((s32[]{:T(128)}, f32[2,8,128]{2,1,0:T(8,128)S(1)}, f32[2,8,3,128]{3,2,1,0:T(4,128)S(1)}, ...), condition=%wide.region_3.4_spmd, body=%wide.region_0.0_spmd.sunk | while | flops 3277826 | bytes 1167461 | solution.py:60
  17.4 0.8 gather_fusion.4
  18.9 0.7 reduce.3
  19.6 0.6 gather_fusion.7
  20.3 0.6 gather_fusion.8
  21.6 4.3 %collective-permute-start = (f32[1,2,5,128]{3,1,0,2:T(2,128)S(1)}, f32[1,2,5,128]{3,1,0,2:T(2,128)S(1)}, u32[]{:S(2)}, u32[]{:S(2)}) collective-permute-start(f32[1,2,5,128]{3,1,0,2:T(2,128)S(1)} %get-tuple-element.362), channel_id=1, source_target_pairs={{0,15},{1,0},{2,1},{3,2},{4,3},{5,4},{6,5},{7,6},{8,7},{9,8},{10,9... | collective-permute-start | bytes 15368 | tf_op jit(solution)/shard_map/ppermute | solution.py:20
  26.0 0.6 gather_fusion.5
  26.6 0.6 gather_fusion.10
  27.2 0.6 collective-permute-start.1
  28.8 4.3 %collective-permute-start.5 = (f32[1,2,5,128]{3,1,0,2:T(2,128)S(1)}, f32[1,2,5,128]{3,1,0,2:T(2,128)S(1)}, u32[]{:S(2)}, u32[]{:S(2)}) collective-permute-start(f32[1,2,5,128]{3,1,0,2:T(2,128)S(1)} %get-tuple-element.357), channel_id=1, source_target_pairs={{0,10},{1,11},{2,12},{3,13},{4,14},{5,15},{6,0},{7,1},{8,2},{9,3},... | collective-permute-start | bytes 15368 | tf_op jit(solution)/shard_map/ppermute | solution.py:20
  33.1 1.4 %collective-permute-start.7 = (f32[1,2,5,128]{3,1,0,2:T(2,128)S(1)}, f32[1,2,5,128]{3,1,0,2:T(2,128)S(1)}, u32[]{:S(2)}, u32[]{:S(2)}) collective-permute-start(f32[1,2,5,128]{3,1,0,2:T(2,128)S(1)} %get-tuple-element.355), channel_id=1, source_target_pairs={{0,8},{1,9},{2,10},{3,11},{4,12},{5,13},{6,14},{7,15},{8,0},{9,1},... | collective-permute-start | bytes 15368 | tf_op jit(solution)/shard_map/ppermute | solution.py:20
  34.6 1.5 %collective-permute-start.8 = (f32[1,2,5,128]{3,1,0,2:T(2,128)S(1)}, f32[1,2,5,128]{3,1,0,2:T(2,128)S(1)}, u32[]{:S(2)}, u32[]{:S(2)}) collective-permute-start(f32[1,2,5,128]{3,1,0,2:T(2,128)S(1)} %get-tuple-element.354), channel_id=1, source_target_pairs={{0,7},{1,8},{2,9},{3,10},{4,11},{5,12},{6,13},{7,14},{8,15},{9,0},... | collective-permute-start | bytes 15368 | tf_op jit(solution)/shard_map/ppermute | solution.py:20
  36.1 2.4 %collective-permute-start.9 = (f32[1,2,5,128]{3,1,0,2:T(2,128)S(1)}, f32[1,2,5,128]{3,1,0,2:T(2,128)S(1)}, u32[]{:S(2)}, u32[]{:S(2)}) collective-permute-start(f32[1,2,5,128]{3,1,0,2:T(2,128)S(1)} %get-tuple-element.353), channel_id=1, source_target_pairs={{0,6},{1,7},{2,8},{3,9},{4,10},{5,11},{6,12},{7,13},{8,14},{9,15},... | collective-permute-start | bytes 15368 | tf_op jit(solution)/shard_map/ppermute | solution.py:20
  38.6 2.3 %collective-permute-start.11 = (f32[1,2,5,128]{3,1,0,2:T(2,128)S(1)}, f32[1,2,5,128]{3,1,0,2:T(2,128)S(1)}, u32[]{:S(2)}, u32[]{:S(2)}) collective-permute-start(f32[1,2,5,128]{3,1,0,2:T(2,128)S(1)} %get-tuple-element.351), channel_id=1, source_target_pairs={{0,4},{1,5},{2,6},{3,7},{4,8},{5,9},{6,10},{7,11},{8,12},{9,13},{1... | collective-permute-start | bytes 15368 | tf_op jit(solution)/shard_map/ppermute | solution.py:20
  40.9 2.1 %collective-permute-start.12 = (f32[1,2,5,128]{3,1,0,2:T(2,128)S(1)}, f32[1,2,5,128]{3,1,0,2:T(2,128)S(1)}, u32[]{:S(2)}, u32[]{:S(2)}) collective-permute-start(f32[1,2,5,128]{3,1,0,2:T(2,128)S(1)} %get-tuple-element.350), channel_id=1, source_target_pairs={{0,3},{1,4},{2,5},{3,6},{4,7},{5,8},{6,9},{7,10},{8,11},{9,12},{10... | collective-permute-start | bytes 15368 | tf_op jit(solution)/shard_map/ppermute | solution.py:20
  43.0 0.8 collective-permute-start.13
  44.0 2.3 %collective-permute-done.12 = f32[1,2,5,128]{3,1,0,2:T(2,128)S(1)} collective-permute-done((f32[1,2,5,128]{3,1,0,2:T(2,128)S(1)}, f32[1,2,5,128]{3,1,0,2:T(2,128)S(1)}, u32[]{:S(2)}, u32[]{:S(2)}) %collective-permute-start.12) | collective-permute-done | bytes 5152 | tf_op jit(solution)/shard_map/ppermute | solution.py:20
  46.4 3.0 %collective-permute-done.13 = f32[1,2,5,128]{3,1,0,2:T(2,128)S(1)} collective-permute-done((f32[1,2,5,128]{3,1,0,2:T(2,128)S(1)}, f32[1,2,5,128]{3,1,0,2:T(2,128)S(1)}, u32[]{:S(2)}, u32[]{:S(2)}) %collective-permute-start.13) | collective-permute-done | bytes 5152 | tf_op jit(solution)/shard_map/ppermute | solution.py:20
  49.8 4.6 %while.41 = (s32[]{:T(128)}, f32[4,8,128]{2,1,0:T(8,128)S(1)}, f32[4,8,3,128]{3,2,1,0:T(4,128)S(1)}, f32[4,8,3,128]{3,2,1,0:T(4,128)S(1)}, f32[4,8,128]{2,1,0:T(8,128)S(1)}, /*index=5*/f32[4,8,128]{2,1,0:T(8,128)S(1)}, s32[]{:T(128)}) while((s32[]{:T(128)}, f32[4,8,128]{2,1,0:T(8,128)S(1)}, f32[4,8,3,128]{3,2,1,0:T(4,128)S(1)}, ...), condition=%wide.region_11.13_spmd, body=%wide.region_8.12_spmd.sunk | while | flops 3277826 | bytes 1167461 | solution.py:60
  54.3 0.7 multiply_divide_fusion
  56.2 1.2 gather_fusion.15
  57.4 4.6 %while.42 = (s32[]{:T(128)}, f32[2,8,3,128]{3,2,1,0:T(4,128)S(1)}, f32[2,8,128]{2,1,0:T(8,128)S(1)}, f32[2,8,128]{2,1,0:T(8,128)S(1)}, f32[2,8,128]{2,1,0:T(8,12...) while((s32[]{:T(128)}, f32[2,8,3,128]{3,2,1,0:T(4,128)S(1)}, ...), condition=%wide.region_15.17_spmd, body=%wide.region_12.16_spmd.sunk | while | flops 6297602 | bytes 2318465 | solution.py:60
  57.9 0.8 multiply_multiply_fusion.28
  58.7 1.0 fusion.97
  60.2 0.8 multiply_multiply_fusion.28
  61.0 1.0 fusion.97
  62.0 3.5 %all-to-all-start.1 = ((f32[16,2,128]{2,1,0:T(2,128)}), f32[16,2,128]{2,1,0:T(2,128)S(1)}, u32[]{:S(2)}, u32[]{:S(2)}) async-start(f32[16,2,128]{2,1,0:T(2,128)} %bitcast.59), calls=%async_computation.1 | async-start | bytes 32768 | tf_op jit(solution)/shard_map/all_to_all | solution.py:118
  65.7 0.6 gather_fusion.14
  66.2 5.8 %all-to-all-done.1 = f32[16,2,128]{2,1,0:T(2,128)S(1)} async-done(((f32[16,2,128]{2,1,0:T(2,128)}), f32[16,2,128]{2,1,0:T(2,128)S(1)}, u32[]{:S(2)}, u32[]{:S(2)}) %all-to-all-start.1) | async-done | bytes 16416 | tf_op jit(solution)/shard_map/all_to_all | solution.py:118
  72.0 9.3 %while.43 = (s32[]{:T(128)}, f32[4,8,3,128]{3,2,1,0:T(4,128)S(1)}, f32[4,8,128]{2,1,0:T(8,128)S(1)}, f32[4,8,128]{2,1,0:T(8,128)S(1)}, f32[4,8,128]{2,1,0:T(8,12...) while((s32[]{:T(128)}, f32[4,8,3,128]{3,2,1,0:T(4,128)S(1)}, ...), condition=%wide.region_19.21_spmd, body=%wide.region_16.20_spmd.sunk | while | flops 6297602 | bytes 2318465 | solution.py:60
  72.5 0.8 multiply_multiply_fusion.30
  73.3 1.0 fusion.99
  74.9 0.8 multiply_multiply_fusion.30
  75.6 1.0 fusion.99
  77.2 0.8 multiply_multiply_fusion.30
  78.0 1.0 fusion.99
  79.5 0.8 multiply_multiply_fusion.30
  80.3 1.0 fusion.99
  81.3 0.8 multiply_reduce_fusion.2
  82.0 0.6 select_reduce_fusion.2
  82.7 38.3 %pmin.7 = f32[]{:T(128)} all-reduce(f32[]{:T(128)} %select_reduce_fusion.2), channel_id=1, replica_groups=mesh['grp'=2,'dom'=16] {'grp','dom'}, use_global_device_ids=true, to_apply=%region_22.24 | all-reduce | flops 1 | bytes 8 | tf_op jit(solution)/shard_map/pmin | solution.py:153
  (160 shorter events, 16.6 us)
Async XLA Ops:
  0.6 11.5 %copy-start = (f32[16,3,128]{2,0,1:T(8,128)S(1)}, f32[16,3,128]{2,0,1:T(8,128)}, u32[]{:S(2)}) copy-start(f32[16,3,128]{2,0,1:T(8,128)} %param.19) | copy-start | bytes 73732
  0.6 11.4 %copy-start.6 = (s32[16,2]{0,1:T(2,128)S(1)}, s32[16,2]{0,1:T(2,128)}, u32[]{:S(2)}) copy-start(s32[16,2]{0,1:T(2,128)} %param.25) | copy-start | bytes 388
  2.4 10.9 %copy-start.2 = (f32[16,128]{1,0:T(8,128)S(1)}, f32[16,128]{1,0:T(8,128)}, u32[]{:S(2)}) copy-start(f32[16,128]{1,0:T(8,128)} %param.20) | copy-start | bytes 24580
  3.9 10.6 %copy-start.4 = (s32[16,128]{1,0:T(8,128)S(1)}, s32[16,128]{1,0:T(8,128)}, u32[]{:S(2)}) copy-start(s32[16,128]{1,0:T(8,128)} %param.24) | copy-start | bytes 24580
  3.9 10.6 %copy-start.3 = (f32[16,128]{1,0:T(8,128)S(1)}, f32[16,128]{1,0:T(8,128)}, u32[]{:S(2)}) copy-start(f32[16,128]{1,0:T(8,128)} %param.22) | copy-start | bytes 24580
  4.6 13.8 %all-to-all-start = ((s32[16,1,2]{2,1,0:T(1,128)}), s32[16,1,2]{2,1,0:T(1,128)S(1)}, u32[]{:S(2)}, u32[]{:S(2)}) async-start(s32[16,1,2]{2,1,0:T(1,128)} %bitcast.42), calls=%async_computation | async-start | bytes 16384 | tf_op jit(solution)/shard_map/all_to_all | solution.py:99
  15.1 2.3 %copy-start.1 = (s32[24,2]{0,1:T(2,128)S(1)}, s32[24,2]{0,1:T(2,128)}, u32[]{:S(2)}) copy-start(s32[24,2]{0,1:T(2,128)} %param.26) | copy-start | bytes 580
  21.6 7.1 %collective-permute-start = (f32[1,2,5,128]{3,1,0,2:T(2,128)S(1)}, f32[1,2,5,128]{3,1,0,2:T(2,128)S(1)}, u32[]{:S(2)}, u32[]{:S(2)}) collective-permute-start(f32[1,2,5,128]{3,1,0,2:T(2,128)S(1)} %get-tuple-element.362), channel_id=1, source_target_pairs={{0,15},{1,0},{2,1},{3,2},{4,3},{5,4},{6,5},{7,6},{8,7},{9,8},{10,9... | collective-permute-start | bytes 15368 | tf_op jit(solution)/shard_map/ppermute | solution.py:20
  27.2 5.9 %collective-permute-start.1 = (f32[1,2,5,128]{3,1,0,2:T(2,128)S(1)}, f32[1,2,5,128]{3,1,0,2:T(2,128)S(1)}, u32[]{:S(2)}, u32[]{:S(2)}) collective-permute-start(f32[1,2,5,128]{3,1,0,2:T(2,128)S(1)} %get-tuple-element.361), channel_id=1, source_target_pairs={{0,14},{1,15},{2,0},{3,1},{4,2},{5,3},{6,4},{7,5},{8,6},{9,7},{10,... | collective-permute-start | bytes 15368 | tf_op jit(solution)/shard_map/ppermute | solution.py:20
  27.8 5.3 %collective-permute-start.2 = (f32[1,2,5,128]{3,1,0,2:T(2,128)S(1)}, f32[1,2,5,128]{3,1,0,2:T(2,128)S(1)}, u32[]{:S(2)}, u32[]{:S(2)}) collective-permute-start(f32[1,2,5,128]{3,1,0,2:T(2,128)S(1)} %get-tuple-element.360), channel_id=1, source_target_pairs={{0,13},{1,14},{2,15},{3,0},{4,1},{5,2},{6,3},{7,4},{8,5},{9,6},{10... | collective-permute-start | bytes 15368 | tf_op jit(solution)/shard_map/ppermute | solution.py:20
  27.9 6.7 %collective-permute-start.3 = (f32[1,2,5,128]{3,1,0,2:T(2,128)S(1)}, f32[1,2,5,128]{3,1,0,2:T(2,128)S(1)}, u32[]{:S(2)}, u32[]{:S(2)}) collective-permute-start(f32[1,2,5,128]{3,1,0,2:T(2,128)S(1)} %get-tuple-element.359), channel_id=1, source_target_pairs={{0,12},{1,13},{2,14},{3,15},{4,0},{5,1},{6,2},{7,3},{8,4},{9,5},{1... | collective-permute-start | bytes 15368 | tf_op jit(solution)/shard_map/ppermute | solution.py:20
  28.5 7.6 %collective-permute-start.4 = (f32[1,2,5,128]{3,1,0,2:T(2,128)S(1)}, f32[1,2,5,128]{3,1,0,2:T(2,128)S(1)}, u32[]{:S(2)}, u32[]{:S(2)}) collective-permute-start(f32[1,2,5,128]{3,1,0,2:T(2,128)S(1)} %get-tuple-element.358), channel_id=1, source_target_pairs={{0,11},{1,12},{2,13},{3,14},{4,15},{5,0},{6,1},{7,2},{8,3},{9,4},{... | collective-permute-start | bytes 15368 | tf_op jit(solution)/shard_map/ppermute | solution.py:20
  28.8 9.7 %collective-permute-start.5 = (f32[1,2,5,128]{3,1,0,2:T(2,128)S(1)}, f32[1,2,5,128]{3,1,0,2:T(2,128)S(1)}, u32[]{:S(2)}, u32[]{:S(2)}) collective-permute-start(f32[1,2,5,128]{3,1,0,2:T(2,128)S(1)} %get-tuple-element.357), channel_id=1, source_target_pairs={{0,10},{1,11},{2,12},{3,13},{4,14},{5,15},{6,0},{7,1},{8,2},{9,3},... | collective-permute-start | bytes 15368 | tf_op jit(solution)/shard_map/ppermute | solution.py:20
  33.1 5.5 %collective-permute-start.6 = (f32[1,2,5,128]{3,1,0,2:T(2,128)S(1)}, f32[1,2,5,128]{3,1,0,2:T(2,128)S(1)}, u32[]{:S(2)}, u32[]{:S(2)}) collective-permute-start(f32[1,2,5,128]{3,1,0,2:T(2,128)S(1)} %get-tuple-element.356), channel_id=1, source_target_pairs={{0,9},{1,10},{2,11},{3,12},{4,13},{5,14},{6,15},{7,0},{8,1},{9,2},... | collective-permute-start | bytes 15368 | tf_op jit(solution)/shard_map/ppermute | solution.py:20
  33.1 7.8 %collective-permute-start.7 = (f32[1,2,5,128]{3,1,0,2:T(2,128)S(1)}, f32[1,2,5,128]{3,1,0,2:T(2,128)S(1)}, u32[]{:S(2)}, u32[]{:S(2)}) collective-permute-start(f32[1,2,5,128]{3,1,0,2:T(2,128)S(1)} %get-tuple-element.355), channel_id=1, source_target_pairs={{0,8},{1,9},{2,10},{3,11},{4,12},{5,13},{6,14},{7,15},{8,0},{9,1},... | collective-permute-start | bytes 15368 | tf_op jit(solution)/shard_map/ppermute | solution.py:20
  34.6 8.4 %collective-permute-start.8 = (f32[1,2,5,128]{3,1,0,2:T(2,128)S(1)}, f32[1,2,5,128]{3,1,0,2:T(2,128)S(1)}, u32[]{:S(2)}, u32[]{:S(2)}) collective-permute-start(f32[1,2,5,128]{3,1,0,2:T(2,128)S(1)} %get-tuple-element.354), channel_id=1, source_target_pairs={{0,7},{1,8},{2,9},{3,10},{4,11},{5,12},{6,13},{7,14},{8,15},{9,0},... | collective-permute-start | bytes 15368 | tf_op jit(solution)/shard_map/ppermute | solution.py:20
  36.1 7.7 %collective-permute-start.9 = (f32[1,2,5,128]{3,1,0,2:T(2,128)S(1)}, f32[1,2,5,128]{3,1,0,2:T(2,128)S(1)}, u32[]{:S(2)}, u32[]{:S(2)}) collective-permute-start(f32[1,2,5,128]{3,1,0,2:T(2,128)S(1)} %get-tuple-element.353), channel_id=1, source_target_pairs={{0,6},{1,7},{2,8},{3,9},{4,10},{5,11},{6,12},{7,13},{8,14},{9,15},... | collective-permute-start | bytes 15368 | tf_op jit(solution)/shard_map/ppermute | solution.py:20
  38.5 5.4 %collective-permute-start.10 = (f32[1,2,5,128]{3,1,0,2:T(2,128)S(1)}, f32[1,2,5,128]{3,1,0,2:T(2,128)S(1)}, u32[]{:S(2)}, u32[]{:S(2)}) collective-permute-start(f32[1,2,5,128]{3,1,0,2:T(2,128)S(1)} %get-tuple-element.352), channel_id=1, source_target_pairs={{0,5},{1,6},{2,7},{3,8},{4,9},{5,10},{6,11},{7,12},{8,13},{9,14},{... | collective-permute-start | bytes 15368 | tf_op jit(solution)/shard_map/ppermute | solution.py:20
  38.6 5.4 %collective-permute-start.11 = (f32[1,2,5,128]{3,1,0,2:T(2,128)S(1)}, f32[1,2,5,128]{3,1,0,2:T(2,128)S(1)}, u32[]{:S(2)}, u32[]{:S(2)}) collective-permute-start(f32[1,2,5,128]{3,1,0,2:T(2,128)S(1)} %get-tuple-element.351), channel_id=1, source_target_pairs={{0,4},{1,5},{2,6},{3,7},{4,8},{5,9},{6,10},{7,11},{8,12},{9,13},{1... | collective-permute-start | bytes 15368 | tf_op jit(solution)/shard_map/ppermute | solution.py:20
  40.9 5.4 %collective-permute-start.12 = (f32[1,2,5,128]{3,1,0,2:T(2,128)S(1)}, f32[1,2,5,128]{3,1,0,2:T(2,128)S(1)}, u32[]{:S(2)}, u32[]{:S(2)}) collective-permute-start(f32[1,2,5,128]{3,1,0,2:T(2,128)S(1)} %get-tuple-element.350), channel_id=1, source_target_pairs={{0,3},{1,4},{2,5},{3,6},{4,7},{5,8},{6,9},{7,10},{8,11},{9,12},{10... | collective-permute-start | bytes 15368 | tf_op jit(solution)/shard_map/ppermute | solution.py:20
  43.0 6.3 %collective-permute-start.13 = (f32[1,2,5,128]{3,1,0,2:T(2,128)S(1)}, f32[1,2,5,128]{3,1,0,2:T(2,128)S(1)}, u32[]{:S(2)}, u32[]{:S(2)}) collective-permute-start(f32[1,2,5,128]{3,1,0,2:T(2,128)S(1)} %get-tuple-element.349), channel_id=1, source_target_pairs={{0,2},{1,3},{2,4},{3,5},{4,6},{5,7},{6,8},{7,9},{8,10},{9,11},{10,... | collective-permute-start | bytes 15368 | tf_op jit(solution)/shard_map/ppermute | solution.py:20
  43.8 5.7 %collective-permute-start.14 = (f32[1,2,5,128]{3,1,0,2:T(2,128)S(1)}, f32[1,2,5,128]{3,1,0,2:T(2,128)S(1)}, u32[]{:S(2)}, u32[]{:S(2)}) collective-permute-start(f32[1,2,5,128]{3,1,0,2:T(2,128)S(1)} %get-tuple-element.348), channel_id=1, source_target_pairs={{0,1},{1,2},{2,3},{3,4},{4,5},{5,6},{6,7},{7,8},{8,9},{9,10},{10,1... | collective-permute-start | bytes 15368 | tf_op jit(solution)/shard_map/ppermute | solution.py:20
  49.7 4.6 %copy-start.5 = (f32[16,128]{1,0:T(8,128)S(1)}, f32[16,128]{1,0:T(8,128)}, u32[]{:S(2)}) copy-start(f32[16,128]{1,0:T(8,128)} %param.21) | copy-start | bytes 24580
  49.7 4.6 %copy-start.7 = (f32[16,128]{1,0:T(8,128)S(1)}, f32[16,128]{1,0:T(8,128)}, u32[]{:S(2)}) copy-start(f32[16,128]{1,0:T(8,128)} %param.23) | copy-start | bytes 24580
  62.0 10.0 %all-to-all-start.1 = ((f32[16,2,128]{2,1,0:T(2,128)}), f32[16,2,128]{2,1,0:T(2,128)S(1)}, u32[]{:S(2)}, u32[]{:S(2)}) async-start(f32[16,2,128]{2,1,0:T(2,128)} %bitcast.59), calls=%async_computation.1 | async-start | bytes 32768 | tf_op jit(solution)/shard_map/all_to_all | solution.py:118
